TPU v7x, 256 devices: a whole 4x4x8 slice. The times are simulated.
256 devices in a mesh: arcs: 16 (over x, y_hi, core), tiles: 16 (over z, y_lo).
Axes of the slice: x: 4, y: 4 (y_hi: 2, y_lo: 2; y = y_hi * 2 + y_lo), z: 8, core: 2. Of those that a mesh axis runs over, the one named last changes fastest.
Arguments:
- design: bfloat16 [24576, 8192], P('arcs', 'tiles'), may hold values from -0.09375 to 0.09375
- observations: float32 [24576], P('arcs'), may hold values from -25 to 25
- solution: float32 [8192], P('tiles'), may hold values from -6 to 6
- arc_ids: int32 [16, 1536], P('arcs'), may hold values from 0 to 3, never falling along the last dimension, each value on 1 to 768 neighbouring positions
- block_live: int32 [16, 12], P('arcs'), may hold values 0 or 1
Outputs:
- normal: float32 [8192, 8192], P('arcs', 'tiles')
- rhs: float32 [8192], P('tiles')
Inputs may be any that keep to these rules, and one draw needn't show every extreme that they name: `arc_ids`: the arcs of a group's rows never fall along its rows; an arc holds at most 768 rows and some arc exactly that many.
All inputs are finite; a program needn't handle non-finite values. No bound on the sum of `block_live` on one device may be relied on, other than what follows from the above.
Results may differ from a plain program's by a relative error of at most 0.0018.
Values may be sent and summed in bfloat16 or wider, within the bound.
A program may use at most 128 MiB of HBM per device.

v0:
```python
import jax
import jax.numpy as jnp
from jax import lax
from jax.sharding import Mesh
from jax.sharding import PartitionSpec as P

ARCS_DEV = 4
TILES = ("tiles_0", "tiles_1")


prior_rows = 4.0


def gathered_by_axis(array, axes, dim):
    for axis in reversed(axes):
        array = lax.all_gather(array, axis, axis=dim, tiled=True)
    return array


def sent_to_all(array, axis):
    count = lax.axis_size(axis)
    return lax.all_to_all(
        jnp.broadcast_to(array[None], (count, *array.shape)), axis, 0, 0, tiled=True
    )


def of_everyone(array, axis):
    return sent_to_all(array, axis).sum(axis=0)


def together(arrays, axis):
    ends = [0]
    for a in arrays:
        ends.append(ends[-1] + a.size)
    total = of_everyone(jnp.concatenate([a.ravel() for a in arrays]), axis)
    return tuple((total[b:e].reshape(a.shape) for a, b, e in zip(arrays, ends, ends[1:])))


def contract_rows(left, right):
    return lax.dot_general(
        left, right, (((0,), (0,)), ((), ())), preferred_element_type=jnp.float32
    )


def local(design, observations, solution, arc_ids, block_live):
    row_count = design.shape[0]
    design_all = gathered_by_axis(design, TILES, 1)
    partial_value = jnp.dot(design.astype(jnp.float32), solution, precision=lax.Precision.HIGHEST)
    predicted = of_everyone(partial_value, TILES)
    residual = observations - predicted
    live_row = (
        jnp.broadcast_to(block_live[0][:, None], (block_live.shape[1], 128))
        .reshape(row_count)
        .astype(jnp.float32)
    )
    arc_match = (arc_ids[0][None, :] == jnp.arange(ARCS_DEV, dtype=jnp.int32)[:, None]).astype(
        jnp.float32
    )
    squares = live_row * residual * residual
    arc_squares = jnp.sum(arc_match * squares[None, :], axis=1)
    arc_counts = jnp.sum(arc_match * live_row[None, :], axis=1)
    totals = together((jnp.sum(arc_squares), jnp.sum(arc_counts)), "arcs")
    variance_all = (totals[0] + 1.0) / (totals[1] + 1.0)
    arc_weight = variance_all / (
        (arc_squares + prior_rows * variance_all) / (arc_counts + prior_rows)
    )
    row_weight = live_row * jnp.sum(arc_match * arc_weight[:, None], axis=0)
    rhs_part = lax.dot_general(
        design.astype(jnp.float32),
        row_weight * residual,
        (((0,), (0,)), ((), ())),
        precision=lax.Precision.HIGHEST,
    )
    weighted = (row_weight[:, None] * design).astype(jnp.bfloat16)
    normal = lax.psum_scatter(
        contract_rows(design_all, weighted), "arcs", scatter_dimension=0, tiled=True
    )
    rhs = of_everyone(rhs_part, "arcs")
    return (normal, rhs)


def solution(mesh):
    finer = Mesh(mesh.devices.reshape(mesh.shape["arcs"], 8, 2), ("arcs", "tiles_0", "tiles_1"))
    return jax.shard_map(
        local,
        mesh=finer,
        in_specs=(P("arcs", TILES), P("arcs"), P(TILES), P("arcs", None), P("arcs", None)),
        out_specs=(P("arcs", TILES), P(TILES)),
        check_vma=False,
    )
```

profile of v0, /device:TPU:1, one launch (start us, length us, event | category | flops | bytes accessed | tf_op | source)
XLA Modules:
  0.0 501.8 jit_solution(8807722876623244042)
XLA Ops:
  7.2 0.0 copy-start
  7.2 0.0 all-gather.3.cloned.1.call-start
  7.2 0.7 all-gather.3.cloned.1.call-update
  7.9 0.0 all-gather.5.cloned.1.call-start
  8.0 55.5 %all-gather.3.cloned.1.call-done = bf16[1536,1024]{1,0:T(8,128)(2,1)} async-done(((bf16[1536,512]{1,0:T(8,128)(2,1)}), bf16[1536,1024]{1,0:T(8,128)(2,1)}) %all-gather.3.cloned.1.call-update) | async-done | bytes 3145744 | tf_op jit(solution)/shard_map/all_gather | solution.py:16
  63.4 0.0 copy-start.1
  63.4 0.0 all-gather.5.cloned.1.call-update
  63.5 0.0 copy-done
  63.5 0.0 copy-start.3
  63.5 0.0 copy-start.4
  63.5 0.0 copy-start.2
  63.5 1.3 copy-done.1
  64.8 1.3 convolution_reduce_fusion
  66.2 0.7 broadcast_in_dim.9
  66.9 6.8 %all-to-all-start = ((f32[16,1,1536]{2,1,0:T(1,128)}), f32[16,1,1536]{2,1,0:T(1,128)S(1)}, u32[]{:S(2)}, u32[]{:S(2)}) async-start(f32[16,1,1536]{2,1,0:T(1,128)} %broadcast_in_dim.9), calls=%async_computation | async-start | bytes 196608 | tf_op jit(solution)/shard_map/all_to_all | solution.py:22
  73.7 0.0 reduce-scatter.2.cloned.1.call-start
  73.8 0.0 copy-done.3
  73.8 0.0 copy-done.4
  73.8 0.1 broadcast_bitcast_fusion
  73.9 8.0 %all-to-all-done = f32[16,1,1536]{2,1,0:T(1,128)S(1)} async-done(((f32[16,1,1536]{2,1,0:T(1,128)}), f32[16,1,1536]{2,1,0:T(1,128)S(1)}, u32[]{:S(2)}, u32[]{:S(2)}) %all-to-all-start) | async-done | bytes 98336 | tf_op jit(solution)/shard_map/all_to_all | solution.py:22
  81.9 0.1 reduce_sum.72
  82.0 0.0 copy-done.2
  82.0 0.1 multiply_multiply_fusion
  82.1 0.6 select_reduce_fusion.3
  82.7 1.4 pad_maximum_fusion
  84.1 15.8 %all_to_all.18 = f32[16,1,2]{2,1,0:T(1,128)S(1)} all-to-all(f32[16,1,2]{2,1,0:T(1,128)S(1)} %broadcast_in_dim.10), channel_id=1, replica_groups=mesh['arcs'=16,'tiles_0'=8,'tiles_1'=2] {'arcs'}, dimensions={0} | all-to-all | bytes 256 | tf_op jit(solution)/shard_map/all_to_all | solution.py:22
  99.9 0.6 fusion.2
  101.8 0.1 select_reduce_fusion.4
  101.9 0.1 fusion.1
  102.0 215.9 %all-gather.5.cloned.1.call-done = bf16[1536,8192]{1,0:T(8,128)(2,1)} async-done(((bf16[1536,1024]{1,0:T(8,128)(2,1)}), bf16[1536,8192]{1,0:T(8,128)(2,1)}) %all-gather.5.cloned.1.call-update) | async-done | bytes 25165840 | tf_op jit(solution)/shard_map/all_gather | solution.py:16
  317.9 21.7 %convolution_bitcast_fusion = f32[8192,512]{0,1:T(8,128)} fusion(bf16[1536,8192]{1,0:T(8,128)(2,1)} %all-gather.5.cloned.1.call-done, bf16[1536,512]{1,0:T(8,128)(2,1)S(1)} %copy-done.1, f32[1536]{0:T(1024)S(1)} %get-tuple-element.15), kind=kOutput, calls=%fused_computation | convolution fusion | flops 12887261184 | bytes 43522048 | tf_op jit(solution)/shard_map/dot_general | solution.py:40
  339.6 0.0 reduce-scatter.2.cloned.1.call-update
  339.7 0.7 fusion.3
  340.4 14.6 %all_to_all.19 = f32[16,1,512]{2,1,0:T(1,128)S(1)} all-to-all(f32[16,1,512]{2,1,0:T(1,128)S(1)} %broadcast_in_dim.11), channel_id=1, replica_groups=mesh['arcs'=16,'tiles_0'=8,'tiles_1'=2] {'arcs'}, dimensions={0} | all-to-all | bytes 65536 | tf_op jit(solution)/shard_map/all_to_all | solution.py:22
  355.0 0.6 reduce_sum.79
  355.7 137.1 %reduce-scatter.2.cloned.1.call-done = f32[512,512]{0,1:T(8,128)} async-done(((f32[8192,512]{0,1:T(8,128)}), f32[512,512]{0,1:T(8,128)}) %reduce-scatter.2.cloned.1.call-update) | async-done | bytes 1048592 | tf_op jit(solution)/shard_map/reduce_scatter | solution.py:75
  492.8 2.5 copy.12
  (7 shorter events, 0.1 us)
Async XLA Ops:
  7.2 56.3 %copy-start = (f32[512]{0:T(512)S(1)}, f32[512]{0:T(512)}, u32[]{:S(2)}) copy-start(f32[512]{0:T(512)} %param.7) | copy-start | bytes 6148
  7.2 56.3 %all-gather.3.cloned.1.call-start = ((), (), s32[]{:S(2)}) async-start(), calls=%async_computation.4 | async-start | bytes 4718592 | tf_op jit(solution)/shard_map/all_gather | solution.py:16
  7.9 310.0 %all-gather.5.cloned.1.call-start = ((), (), s32[]{:S(2)}) async-start(), calls=%async_computation.5 | async-start | bytes 28311552 | tf_op jit(solution)/shard_map/all_gather | solution.py:16
  63.4 1.4 copy-start.1
  63.5 10.3 %copy-start.3 = (s32[1,1536]{1,0:T(1,128)S(1)}, s32[1,1536]{1,0:T(1,128)}, u32[]{:S(2)}) copy-start(s32[1,1536]{1,0:T(1,128)} %param.8) | copy-start | bytes 18436
  63.5 10.3 %copy-start.4 = (s32[1,12]{1,0:T(1,128)S(1)}, s32[1,12]{1,0:T(1,128)}, u32[]{:S(2)}) copy-start(s32[1,12]{1,0:T(1,128)} %param.9) | copy-start | bytes 148
  63.5 18.5 %copy-start.2 = (f32[1536]{0:T(1024)S(1)}, f32[1536]{0:T(1024)}, u32[]{:S(2)}) copy-start(f32[1536]{0:T(1024)} %param.6) | copy-start | bytes 18436
  66.9 15.0 %all-to-all-start = ((f32[16,1,1536]{2,1,0:T(1,128)}), f32[16,1,1536]{2,1,0:T(1,128)S(1)}, u32[]{:S(2)}, u32[]{:S(2)}) async-start(f32[16,1,1536]{2,1,0:T(1,128)} %broadcast_in_dim.9), calls=%async_computation | async-start | bytes 196608 | tf_op jit(solution)/shard_map/all_to_all | solution.py:22
  73.7 419.1 %reduce-scatter.2.cloned.1.call-start = ((), (), s32[]{:S(2)}) async-start(), calls=%async_computation.6 | async-start | bytes 17825792 | tf_op jit(solution)/shard_map/reduce_scatter | solution.py:75
Sparse Core Ops, SparseCore 0:
  9.8 53.6 all-gather.2
  65.2 252.6 all-gather.4
  339.8 152.9 reduce-scatter.1
where the time goes:
time: 502 us
  waiting for transfers between devices  417 us (83%)
  blocking collectives  30.4 us (6%)
  matrix products  23.8 us (5%)
  between operations  15.2 us (3%)
  starting transfers between devices  6.95 us (1%)
  local copies, waits for them, and re-layouts  5.29 us (1%)
    all_gather x2, waiting for transfers between devices, gathered_by_axis(): array = lax.all_gather(array, axis, axis=dim, tiled=True)  271 us
    reduce_scatter x1, waiting for transfers between devices, local(): lax.psum_scatter(contract_rows(design_all, weighted), 'arcs', scatter_dim...  137 us
    all_to_all x2, blocking collectives, sent_to_all(): lax.all_to_all(jnp.broadcast_to(array[None], (count, *array.shape)), axis...  30.4 us
    dot_general x1, matrix products, contract_rows(): lax.dot_general(left, right, (((0,), (0,)), ((), ())), preferred_element_...  21.7 us
  transfers between devices with their start and end apart: 4, of which 4 were waited for; matrix products, arithmetic and copies ran while one was open for 1% of the time, Pallas kernels for 0%

commit v1 on v0

v1 whole, which is shorter than its diff:
```python
import functools

import jax
import jax.numpy as jnp
from jax import lax
from jax.experimental import pallas as pl
from jax.experimental.pallas import tpu as pltpu
from jax.sharding import PartitionSpec as P

MESH = pl.DeviceIdType.MESH
F32 = jnp.float32
BF16 = jnp.bfloat16

ARCS_DEV = 4
PRIOR = 4.0
ROWS = 1536
COLS = 512
CHUNKS = 12
STEP = ROWS // CHUNKS
PEERS = 15
N = 10
LEAD = 6
EXACT = 3
PAIRS = (
    (0, 0, False),
    (3, 0, True),
    (3, 1, True),
    (3, 2, True),
    (4, 2, False),
    (2, 5, False),
    (1, 5, True),
    (0, 5, True),
    (3, 5, True),
    (4, 5, False),
)
SCALED = {0: 0, 1: 1, 2: 2, 5: 3}
LATE = (6, 7, 8, 5, 9)
MOVED = [
    sum(bool(PAIRS[p][0]) for p in batch) + sum(bool(PAIRS[p][1]) for p in batch if PAIRS[p][2])
    for batch in ((0, 1, 2, 3, 4), (6, 7, 8), (5, 9))
]


def parts_of(row, height):
    first = row.astype(BF16).astype(F32)
    rest = row - first
    second = rest.astype(BF16).astype(F32)
    third = (rest - second).astype(BF16).astype(F32)
    at = lax.broadcasted_iota(jnp.int32, (height, row.shape[1]), 0)
    zero = jnp.zeros((), F32)
    return jnp.where(
        at == 0, first, jnp.where(at == 1, second, jnp.where(at == 2, third, zero))
    ).astype(BF16)


def kernel(
    live_ref, design, obs_ref, sol_ref, ids_ref, out_ref, rhs_ref,
    below, below2, above, above2, across2, turned, plain, scaled, weight_row, weight_column,
    pred_all, sig_all, rhs_all, partial, from_core,
    one_out, one_in, two_out, two_in, two_own, three_out, three_in,
    spread_out, spread_in, own_piece, whole_all, moved,
    g_send, g_recv, small_send, small_recv, c_send, c_recv, one_send, one_recv,
    two_send, two_recv, three_send, three_recv, s_send, s_recv, m_send, m_recv, f_send, f_recv, l_sem,
):
    a = lax.axis_index("arcs")
    t = lax.axis_index("tiles")
    x, yh, c = a // 4, (a // 2) % 2, a % 2
    z, yl = t // 2, t % 2
    up = ((z + 1) % 8) * 2 + yl
    down = ((z + 7) % 8) * 2 + yl
    beside = z * 2 + (1 - yl)
    blocks = (design, below, below2, above, above2, across2)
    names = (
        t,
        down,
        ((z + 6) % 8) * 2 + yl,
        up,
        ((z + 2) % 8) * 2 + yl,
        ((z + 6) % 8) * 2 + (1 - yl),
    )
    near = x + 1 - 2 * (x % 2)
    far = 3 - x
    opposite = 3 - near

    barrier = pltpu.get_barrier_semaphore()
    for r in range(1, 16):
        pl.semaphore_signal(barrier, inc=1, device_id=(a, (t + r) % 16), device_id_type=MESH)
        pl.semaphore_signal(barrier, inc=1, device_id=((a + r) % 16, t), device_id_type=MESH)

    taps = parts_of(sol_ref[...], 16)
    for k in range(0, ROWS, 256):
        rows = slice(k, k + 256)
        value = lax.dot_general(
            taps, design[rows, :], (((1,), (1,)), ((), ())), preferred_element_type=F32
        )
        pred_all[t, :, rows] = jnp.sum(value, axis=0, keepdims=True)
    pl.semaphore_wait(barrier, 2 * PEERS)

    streams = (
        (design, below, up),
        (design, above, down),
        (below, below2, up),
        (above, above2, down),
        (below2, across2, beside),
    )

    def gather(s, k):
        src, dst, tile = streams[s]
        rows = pl.ds(k * STEP, STEP)
        return pltpu.make_async_remote_copy(
            src_ref=src.at[rows], dst_ref=dst.at[rows],
            send_sem=g_send.at[s], recv_sem=g_recv.at[s, k],
            device_id=(a, tile), device_id_type=MESH,
        )

    def small(buffer, me, which, device):
        return pltpu.make_async_remote_copy(
            src_ref=buffer.at[me], dst_ref=buffer.at[me],
            send_sem=small_send.at[which], recv_sem=small_recv.at[which],
            device_id=device, device_id_type=MESH,
        )

    def small_all(buffer, which):
        every = buffer.at[pl.ds(0, PEERS)]
        return pltpu.make_async_remote_copy(
            src_ref=every, dst_ref=every,
            send_sem=small_send.at[which], recv_sem=small_recv.at[which],
            device_id=(a, beside), device_id_type=MESH,
        )

    gather(0, 0).start()
    gather(1, 0).start()
    for r in range(1, 16):
        small(pred_all, t, 0, (a, (t + r) % 16)).start()
    for k in range(1, CHUNKS):
        if k < LEAD:
            gather(0, k).start()
        gather(1, k).start()

    def pass_up(k):
        gather(0, k).wait_recv()
        gather(2, k).start()
        if k + LEAD < CHUNKS:
            gather(0, k + LEAD).start()

    small_all(pred_all, 0).wait_recv()
    pass_up(0)
    pass_up(1)
    predicted = pred_all[0]
    for i in range(1, 16):
        predicted = predicted + pred_all[i]
    observed = jnp.concatenate([obs_ref[i : i + 1, :] for i in range(12)], axis=1)
    residual = observed - predicted
    live = jnp.concatenate(
        [jnp.full((1, 128), live_ref[0, i].astype(F32), F32) for i in range(12)], axis=1
    )
    squares = live * residual * residual
    ids = ids_ref[...]
    matches = [(ids == k).astype(F32) for k in range(ARCS_DEV)]
    arc_squares = [jnp.sum(m * squares, axis=1, keepdims=True) for m in matches]
    arc_counts = [jnp.sum(m * live, axis=1, keepdims=True) for m in matches]
    sig_all[a, :, 0:128] = jnp.broadcast_to(sum(arc_squares[1:], arc_squares[0]), (1, 128))
    sig_all[a, :, 128:256] = jnp.broadcast_to(sum(arc_counts[1:], arc_counts[0]), (1, 128))
    for r in range(1, 16):
        small(sig_all, a, 1, ((a + r) % 16, t)).start()
    small_all(sig_all, 1).wait_recv()
    pass_up(2)
    pass_up(3)
    totals = sig_all[0]
    for i in range(1, 16):
        totals = totals + sig_all[i]
    sigma = (totals[:, 0:1] + 1.0) / (totals[:, 128:129] + 1.0)
    row_weight = jnp.zeros((1, ROWS), F32)
    for m, s, n in zip(matches, arc_squares, arc_counts):
        row_weight = row_weight + m * (sigma / ((s + PRIOR * sigma) / (n + PRIOR)))
    row_weight = live * row_weight
    weight_row[...] = row_weight
    rhs_part = lax.dot_general(
        parts_of(row_weight * residual, 16), design[...],
        (((1,), (0,)), ((), ())), preferred_element_type=F32,
    )
    rhs_all[a] = jnp.sum(rhs_part, axis=0, keepdims=True)
    for r in range(1, 16):
        small(rhs_all, a, 2, ((a + r) % 16, t)).start()

    for i in range(0, ROWS, 128):
        tile = jnp.broadcast_to(row_weight[:, i : i + 128], (128, 128))
        weight_column[i : i + 128, :] = tile.T

    def turn(q, k):
        block = blocks[q]
        rows = slice(k * STEP, (k + 1) * STEP)
        tile = block[rows, :].T
        plain[q, :, rows] = tile
        turned[q, :, rows] = (tile.astype(F32) * weight_row[:, rows]).astype(BF16)

    def scale(v, k):
        block, n = blocks[v], SCALED[v]
        rows = slice(k * STEP, (k + 1) * STEP)
        for j in range(0, COLS, 128):
            tile = block[rows, j : j + 128].astype(F32) * weight_column[rows, :]
            scaled[n, rows, j : j + 128] = tile.astype(BF16)

    def product(p, lo, hi):
        q, v, _ = PAIRS[p]
        n, block = SCALED[v], blocks[v]
        for i in range(0, COLS, 256):
            cols = slice(i, i + 256)
            value = jnp.dot(turned[q, :, lo:hi], block[lo:hi, cols], preferred_element_type=F32)
            value = value + jnp.dot(
                plain[q, :, lo:hi], scaled[n, lo:hi, cols], preferred_element_type=F32
            )
            value = 0.5 * value
            for half in (0, 1):
                rows = slice(half * 256, half * 256 + 256)
                if lo:
                    partial[p, half, :, cols] += value[rows, :]
                else:
                    partial[p, half, :, cols] = value[rows, :]

    def core_copy(p):
        return pltpu.make_async_remote_copy(
            src_ref=partial.at[p, 1 - c], dst_ref=from_core.at[p],
            send_sem=c_send.at[0], recv_sem=c_recv.at[p],
            device_id=(x * 4 + yh * 2 + (1 - c), t), device_id_type=MESH,
        )

    def multiply(p, lo, hi):
        product(p, lo, hi)
        if hi == ROWS:
            core_copy(p).start()

    def at(i):
        return pl.ds(pl.multiple_of(i * 128, 128), 128)

    def both(p, half, strip):
        rows = slice(half * 128, half * 128 + 128)
        return partial[p, c, rows, at(strip)] + from_core[p, rows, at(strip)]

    def first_copy(p, half):
        pieces = pl.ds(2 * half, 2)
        return pltpu.make_async_remote_copy(
            src_ref=one_out.at[p, pieces], dst_ref=one_in.at[p, pieces],
            send_sem=one_send.at[0], recv_sem=one_recv.at[p, half],
            device_id=((far if half else near) * 4 + yh * 2 + c, t), device_id_type=MESH,
        )

    def second_copy(p, half):
        return pltpu.make_async_remote_copy(
            src_ref=two_out.at[p, half], dst_ref=two_in.at[p, half],
            send_sem=two_send.at[0], recv_sem=two_recv.at[p, half],
            device_id=((near if half else far) * 4 + yh * 2 + c, t), device_id_type=MESH,
        )

    def third_copy(p):
        return pltpu.make_async_remote_copy(
            src_ref=three_out.at[p], dst_ref=three_in.at[p],
            send_sem=three_send.at[0], recv_sem=three_recv.at[p],
            device_id=(x * 4 + (1 - yh) * 2 + c, t), device_id_type=MESH,
        )

    def first(p):
        core_copy(p).wait_recv()
        for half, neighbour in ((0, near), (1, far)):
            one_out[p, 2 * half] = both(p, half, neighbour)
            one_out[p, 2 * half + 1] = both(p, half, opposite)
            first_copy(p, half).start()

    def second(p):
        for half, neighbour in ((0, far), (1, near)):
            first_copy(p, half).wait_recv()
            two_out[p, half] = both(p, half, neighbour) + one_in[p, 2 * half + 1]
            second_copy(p, half).start()
            two_own[p, half] = both(p, half, x) + one_in[p, 2 * half]

    def third(p):
        for half in (0, 1):
            second_copy(p, half).wait_recv()
        three_out[p] = two_own[p, 1 - yh] + two_in[p, 1 - yh]
        third_copy(p).start()
        own_piece[p] = two_own[p, yh] + two_in[p, yh]

    place = x * 2 + yh

    def spread_copy(p, r):
        peer = (place + r) % 8
        return pltpu.make_async_remote_copy(
            src_ref=spread_out.at[p - EXACT, peer], dst_ref=spread_in.at[p - EXACT, r - 1],
            send_sem=s_send.at[0], recv_sem=s_recv.at[p - EXACT],
            device_id=((peer // 2) * 4 + (peer % 2) * 2 + c, t), device_id_type=MESH,
        )

    def spread(p):
        core_copy(p).wait_recv()
        for i in range(4):
            for j in (0, 1):
                rows, cols = slice(j * 128, j * 128 + 128), slice(i * 128, i * 128 + 128)
                total = partial[p, c, rows, cols] + from_core[p, rows, cols]
                spread_out[p - EXACT, i * 2 + j] = total.astype(BF16)
        for r in range(1, 8):
            spread_copy(p, r).start()
        own_piece[p] = partial[p, c, at(yh), at(x)] + from_core[p, at(yh), at(x)]

    row_at = pl.multiple_of(c * 256 + yh * 128, 128)
    col_at = pl.multiple_of(x * 128, 128)

    def all_of(ref, sem, send):
        copy = pltpu.make_async_remote_copy(
            src_ref=ref, dst_ref=ref, send_sem=sem, recv_sem=sem,
            device_id=(a, beside), device_id_type=MESH,
        )
        if send:
            copy.wait_send()
        else:
            copy.wait_recv()

    def outputs(p):
        q, v, mirrored = PAIRS[p]
        return [(p, q, -p % 5 and 8 - p % 5)] + ([(N + p, 2 if v == 5 else v, p % 5)] if mirrored else [])

    def batch(p):
        return 0 if p < 5 else 1 + (p in (5, 9))

    def tile_copy(n, column, group, dz, part):
        return pltpu.make_async_remote_copy(
            src_ref=whole_all.at[n], dst_ref=moved.at[group, dz],
            send_sem=m_send.at[0], recv_sem=m_recv.at[part],
            device_id=(a, names[column]), device_id_type=MESH,
        )

    def deliver(p):
        total = own_piece[p]
        if p < EXACT:
            third_copy(p).wait_recv()
            total = total + three_in[p]
        else:
            all_of(spread_in.at[p - EXACT], s_recv.at[p - EXACT], False)
            for r in range(7):
                total = total + spread_in[p - EXACT, r].astype(F32)
        for n, column, dz in outputs(p):
            value = total.T if n < N else total
            if column:
                whole_all[n] = value
                tile_copy(n, column, p // 5, dz, batch(p)).start()
            else:
                moved[p // 5, dz] = value

    def settle(part):
        group = min(part, 1)
        all_of(moved.at[group, pl.ds(0, MOVED[part])], m_recv.at[part], False)
        for r in range(8):
            row = (place + r) % 8
            dz = (row + 8 - z) % 8
            due = True if part == 0 else (dz % 4 == 0) == (part == 2)
            mirrored = jnp.logical_and(dz >= 1, dz <= 3)
            r0 = pl.multiple_of(jnp.where(mirrored, row_at, col_at), 128)
            c0 = pl.multiple_of(jnp.where(mirrored, col_at, row_at), 128)
            side = yl if group == 0 else jnp.where(mirrored, yl, 1 - yl)
            tile = t if group == 0 else jnp.where(mirrored, beside, t)
            source = moved.at[group, dz]
            target = out_ref.at[pl.ds(r0, 128), pl.ds(c0, 128)]

            def away():
                pltpu.make_async_remote_copy(
                    src_ref=source, dst_ref=target,
                    send_sem=f_send.at[0], recv_sem=f_recv.at[0],
                    device_id=(row * 2 + side, tile), device_id_type=MESH,
                ).start()

            if r:
                pl.when(due)(away)
            else:
                here = side == c
                if group:
                    here = jnp.logical_and(here, jnp.logical_not(mirrored))

                @pl.when(jnp.logical_and(due, here))
                def _():
                    keep = pltpu.make_async_copy(source, target, l_sem.at[0])
                    keep.start()
                    keep.wait()

                pl.when(jnp.logical_and(due, jnp.logical_not(here)))(away)

    def rhs_total():
        small_all(rhs_all, 2).wait_recv()
        rhs = rhs_all[0]
        for i in range(1, 16):
            rhs = rhs + rhs_all[i]
        for i in range(4):
            rhs_ref[i : i + 1, :] = rhs[:, i * 128 : i * 128 + 128]

    def arrive(s, k):
        gather(s, k).wait_recv()

    plan = []

    def add(when, task, *args):
        plan.append((when, len(plan), task, args))

    unit, start = 2.97, 8.0
    order = [("own", k) for k in range(LEAD)]
    for k in range(CHUNKS):
        order.append(("on", k))
        if k + LEAD < CHUNKS:
            order.append(("own", k + LEAD))
    landed = {item: start + unit * (i + 1) for i, item in enumerate(order)}
    weights = 26.0
    for k in range(CHUNKS):
        own, on = landed["own", k], landed["on", k]
        straight = start + unit * (k + 1)
        straight_on = straight + unit * CHUNKS
        if k > 3:
            add(own, pass_up, k)
        add(straight, arrive, 1, k)
        add(straight, lambda k: gather(3, k).start(), k)
        add(on, arrive, 2, k)
        add(on, lambda k: gather(4, k).start(), k)
        add(straight_on, arrive, 3, k)
        add(on + unit + 2.0, arrive, 4, k)
        add(weights, turn, 0, k)
        add(weights, scale, 0, k)
        add(max(weights, own) + 0.2, turn, 1, k)
        add(max(weights, own) + 0.2, scale, 1, k)
        add(max(weights, straight) + 0.2, turn, 3, k)
        add(max(weights, on) + 0.2, turn, 2, k)
        add(max(weights, on) + 0.2, scale, 2, k)
        add(straight_on + 0.2, turn, 4, k)
        add(on + unit + 2.2, scale, 5, k)

    def last(kind, k):
        return landed[kind, k]

    end = landed["on", CHUNKS - 1]
    add(weights + 1, multiply, 0, 0, ROWS)
    add(start + unit * CHUNKS + 0.5, multiply, 1, 0, ROWS)
    add(last("own", CHUNKS - 1) + 0.5, multiply, 2, 0, ROWS)
    for p in (3, 4):
        add(last("on", 8) + 0.5 + p / 10, multiply, p, 0, 1152)
        add(end + 0.3 + p / 10, multiply, p, 1152, ROWS)
    late = end + unit + 2.2
    for p in range(5, N):
        add(last("on", 5) + unit + 2.5 + p / 2, multiply, p, 0, 768)
        add(last("on", 9) + unit + 2.5 + p / 10, multiply, p, 768, 1280)
        add(late + LATE.index(p) / 100, multiply, p, 1280, ROWS)
    ready = (weights + 3, start + unit * CHUNKS + 2, last("own", 11) + 2)
    for p in range(EXACT):
        for i, stage in enumerate((first, second, third, deliver)):
            add(ready[p] + 2 + 6 * i, stage, p)
    for p in (3, 4):
        add(end + 2 + 0.4 * (p - 3), spread, p)
        add(end + 11.2 + 0.4 * (p - 3), deliver, p)
    for i, p in enumerate(LATE):
        add(late + 1.6 + 0.9 * i, spread, p)
        add(end + 13.5 + 2.8 * i, deliver, p)
    add(end + 13.6 + 2.8 * 2, settle, 0)
    add(end + 50, settle, 1)
    add(end + 51, settle, 2)
    add(end + 1, rhs_total)
    for _, _, task, args in sorted(plan, key=lambda item: item[:2]):
        task(*args)

    for s in range(5):
        all_of(design, g_send.at[s], True)
    small_all(pred_all, 0).wait_send()
    small_all(sig_all, 1).wait_send()
    small_all(rhs_all, 2).wait_send()
    all_of(from_core, c_send.at[0], True)
    all_of(one_out, one_send.at[0], True)
    all_of(two_out, two_send.at[0], True)
    all_of(spread_in, s_send.at[0], True)
    all_of(three_out, three_send.at[0], True)
    all_of(whole_all.at[pl.ds(0, sum(MOVED))], m_send.at[0], True)
    gap = (place + 8 - z) % 8
    crossed = jnp.logical_and(c != yl, jnp.logical_and(gap >= 1, gap <= 3))

    def settled(count):
        every = whole_all.at[pl.ds(0, count)]
        all_of(every, f_send.at[0], True)
        all_of(every, f_recv.at[0], False)

    pl.when(crossed)(lambda: settled(16))
    pl.when(jnp.logical_not(crossed))(lambda: settled(15))


def local(design, observations, solution, arc_ids, block_live):
    vmem = pl.BlockSpec(memory_space=pltpu.VMEM)
    normal, rhs = pl.pallas_call(
        kernel,
        out_shape=(
            jax.ShapeDtypeStruct((COLS, COLS), F32),
            jax.ShapeDtypeStruct((4, 128), F32),
        ),
        in_specs=[pl.BlockSpec(memory_space=pltpu.SMEM)] + [vmem] * 4,
        out_specs=(pl.BlockSpec(memory_space=pltpu.HBM), vmem),
        scratch_shapes=[pltpu.VMEM((ROWS, COLS), BF16)] * 5
        + [
            pltpu.VMEM((5, COLS, ROWS), BF16),
            pltpu.VMEM((5, COLS, ROWS), BF16),
            pltpu.VMEM((4, ROWS, COLS), BF16),
            pltpu.VMEM((1, ROWS), F32),
            pltpu.VMEM((ROWS, 128), F32),
            pltpu.VMEM((16, 1, ROWS), F32),
            pltpu.VMEM((16, 1, 256), F32),
            pltpu.VMEM((16, 1, COLS), F32),
        ]
        + [pltpu.VMEM((N, 2, 256, COLS), F32), pltpu.VMEM((N, 256, COLS), F32)]
        + [pltpu.VMEM((EXACT, 4, 128, 128), F32)] * 2
        + [pltpu.VMEM((EXACT, 2, 128, 128), F32)] * 3
        + [pltpu.VMEM((EXACT, 128, 128), F32)] * 2
        + [
            pltpu.VMEM((N - EXACT, 8, 128, 128), BF16),
            pltpu.VMEM((N - EXACT, 7, 128, 128), BF16),
            pltpu.VMEM((N, 128, 128), F32),
        ]
        + [pltpu.VMEM((2 * N, 128, 128), F32), pltpu.VMEM((2, 8, 128, 128), F32)]
        + [
            pltpu.SemaphoreType.DMA((5,)),
            pltpu.SemaphoreType.DMA((5, CHUNKS)),
            pltpu.SemaphoreType.DMA((3,)),
            pltpu.SemaphoreType.DMA((3,)),
            pltpu.SemaphoreType.DMA((1,)),
            pltpu.SemaphoreType.DMA((N,)),
            pltpu.SemaphoreType.DMA((1,)),
            pltpu.SemaphoreType.DMA((EXACT, 2)),
            pltpu.SemaphoreType.DMA((1,)),
            pltpu.SemaphoreType.DMA((EXACT, 2)),
            pltpu.SemaphoreType.DMA((1,)),
            pltpu.SemaphoreType.DMA((EXACT,)),
            pltpu.SemaphoreType.DMA((1,)),
            pltpu.SemaphoreType.DMA((N - EXACT,)),
            pltpu.SemaphoreType.DMA((1,)),
            pltpu.SemaphoreType.DMA((3,)),
            pltpu.SemaphoreType.DMA((1,)),
            pltpu.SemaphoreType.DMA((1,)),
            pltpu.SemaphoreType.DMA((1,)),
        ],
        compiler_params=pltpu.CompilerParams(
            collective_id=0, has_side_effects=True, vmem_limit_bytes=60 * 1024 * 1024
        ),
        name="normal_equations",
    )(
        block_live,
        design,
        observations.reshape(12, 128),
        solution.reshape(1, COLS),
        arc_ids,
    )
    return normal, rhs.reshape(COLS)


def solution(mesh):
    return jax.shard_map(
        local,
        mesh=mesh,
        in_specs=(P("arcs", "tiles"), P("arcs"), P("tiles"), P("arcs", None), P("arcs", None)),
        out_specs=(P("arcs", "tiles"), P("tiles")),
        check_vma=False,
    )
```

time: 502 us -> 135 us (0.27)
  waiting for transfers between devices: 417 us -> 0 us
  Pallas kernels: 0 us -> 131 us
  blocking collectives: 30.4 us -> 0 us
  matrix products: 23.8 us -> 0 us
  between operations: 15.2 us -> 0.65 us
  starting transfers between devices: 6.95 us -> 0 us
    all_gather x2 -> x0, waiting for transfers between devices: 271 us -> none  [gathered_by_axis(): array = lax.all_gather(array, axis, axis=dim, tiled=True)]
    reduce_scatter x1 -> x0, waiting for transfers between devices: 137 us -> none  [local(): lax.psum_scatter(contract_rows(design_all, weighted), 'arcs', scatter_dim...]
    pallas_call x0 -> x1, Pallas kernels: none -> 131 us  [local(): pl.pallas_call(kernel, out_shape=(jax.ShapeDtypeStruct((COLS, COLS), F32)...]
    all_to_all x2 -> x0, blocking collectives: 30.4 us -> none  [sent_to_all(): lax.all_to_all(jnp.broadcast_to(array[None], (count, *array.shape)), axis...]
    dot_general x3 -> x0, matrix products: 23.8 us -> none  [the longest x1 21.7 us: contract_rows(): lax.dot_general(left, right, (((0,), (0,)), ((), ())), preferred_element_...]
    all_to_all x1 -> x0, waiting for transfers between devices: 8.02 us -> none  [sent_to_all(): lax.all_to_all(jnp.broadcast_to(array[None], (count, *array.shape)), axis...]
    all_to_all x1 -> x0, starting transfers between devices: 6.84 us -> none  [sent_to_all(): lax.all_to_all(jnp.broadcast_to(array[None], (count, *array.shape)), axis...]
  transfers between devices with their start and end apart: 4 -> 0, of which waited for: 4 -> 0; matrix products, arithmetic and copies ran while one was open for 1% -> 0% of each run, Pallas kernels for 0% -> 0%
where the time goes in v1:
time: 135 us
  Pallas kernels  131 us (97%)
  local copies, waits for them, and re-layouts  2.85 us (2%)
    pallas_call x1, Pallas kernels, local(): pl.pallas_call(kernel, out_shape=(jax.ShapeDtypeStruct((COLS, COLS), F32)...  131 us
    unnamed x4, local copies, waits for them, and re-layouts  2.85 us

profile of v1, /device:TPU:1, one launch (start us, length us, event | category | flops | bytes accessed | tf_op | source)
XLA Modules:
  0.0 134.7 jit_solution(6267335398423151002)
XLA Ops:
  0.6 131.2 %normal_equations.1 = (f32[512,512]{1,0:T(8,128)}, f32[4,128]{1,0:T(4,128)}) custom-call(s32[1,12]{1,0:T(1,128)} %live_ref.1, bf16[1536,512]{1,0:T(8,128)(2,1)} %design.1, f32[12,128]{1,0:T(8,128)} %bitcast.3, f32[1,512]{1,0:T(1,128)} %bitcast.4, s32[1,1536]{1,0:T(1,128)} %ids_ref.1), custom_call_target="tpu_custom_call" | custom-call | tf_op jit(solution)/shard_map/normal_equations/pallas_call | solution.py:488
  131.8 0.0 copy-start
  131.8 2.3 %copy.9 = f32[512,512]{1,0:T(8,128)} copy(f32[512,512]{1,0:T(8,128)} %get-tuple-element.8) | data formatting | bytes 2097152
  134.1 0.0 copy-done
  134.1 0.6 copy.10
Async XLA Ops:
  131.8 2.3 %copy-start = (f32[4,128]{1,0:T(4,128)S(1)}, f32[4,128]{1,0:T(4,128)}, u32[]{:S(2)}) copy-start(f32[4,128]{1,0:T(4,128)} %get-tuple-element.5) | copy-start | bytes 6148
